TPU v7x, 32 devices: a whole 2x2x4 slice. The times are simulated.
32 devices in a mesh: gz: 2 (over core), row: 4 (over y, x), col: 4 (over z).
Axes of the slice: x: 2, y: 2, z: 4, core: 2. Of those that a mesh axis runs over, the one named last changes fastest.
Arguments:
- rhs_sub: float32 [2, 3, 4, 96, 256], P('gz', None, 'row', 'col'), may hold values from -6 to 6
- rhs_top: float32 [2, 4, 96, 256], P(None, 'row', 'col'), may hold values from -6 to 6
- lower_sub: bfloat16 [2, 3, 4, 4, 256, 256], P('gz', None, 'row', 'col'), may hold values from -0.078125 to 0.078125
- lower_link: bfloat16 [2, 2, 4, 4, 256, 256], P('gz', None, 'row', 'col'), may hold values from -0.078125 to 0.078125
- lower_top: bfloat16 [1, 4, 4, 256, 256], P(None, 'row', 'col'), may hold values from -0.078125 to 0.078125
- inv_sub: bfloat16 [2, 3, 4, 256, 256], P('gz', None, 'row'), may hold values from -0.3 to 1.3
- inv_top: bfloat16 [2, 4, 256, 256], P(None, 'row'), may hold values from -0.3 to 1.3
- mask_sub: int32 [2, 3, 4, 4], P('gz', None, 'row', 'col'), may hold values 0 or 1
- mask_link: int32 [2, 2, 4, 4], P('gz', None, 'row', 'col'), may hold values 0 or 1
- mask_top: int32 [1, 4, 4], P(None, 'row', 'col'), may hold values 0 or 1
Outputs:
- sol_sub: float32 [2, 3, 4, 96, 256], P('gz', None, 'row', 'col')
- sol_top: float32 [2, 4, 96, 256], P(None, 'row', 'col')
All inputs are finite; a program needn't handle non-finite values. No bound on the sum of `mask_sub` or of `mask_link` or of `mask_top` on one device may be relied on, other than what follows from the above.
Results may differ from a plain program's by a relative error of at most 0.02.
Values may be sent and summed in bfloat16 or wider, within the bound.
A program may use at most 64 MiB of HBM per device.

v0:
```python
import jax
import jax.numpy as jnp
from jax import lax
from jax.sharding import PartitionSpec as P


def forward_terms(column_vectors, blocks, pattern):
    product = jnp.einsum(
        "jnb,ijbd->ijnd", column_vectors, blocks, preferred_element_type=jnp.float32
    )
    return jnp.sum(product * pattern.astype(jnp.float32)[:, :, None, None], axis=1)


def backward_terms(row_vectors, blocks, pattern):
    product = jnp.einsum("knd,kjbd->kjnb", row_vectors, blocks, preferred_element_type=jnp.float32)
    return jnp.sum(product * pattern.astype(jnp.float32)[:, :, None, None], axis=0)


def inverse_rows(residual, inverse):
    return jnp.einsum(
        "inb,ibd->ind", residual.astype(jnp.bfloat16), inverse, preferred_element_type=jnp.float32
    )


def inverse_cols(residual, inverse):
    return jnp.einsum(
        "ind,ibd->inb", residual.astype(jnp.bfloat16), inverse, preferred_element_type=jnp.float32
    )


def own_share(values, share_cols):
    return lax.dynamic_slice_in_dim(values, lax.axis_index("col") * share_cols, share_cols, 1)


def level_solve(partial_sum, rhs_local, inverse, gate_value, across_groups):
    share_cols = rhs_local.shape[1]
    col_index = lax.axis_index("col")
    placed = lax.dynamic_update_slice_in_dim(
        jnp.zeros_like(partial_sum), rhs_local * gate_value, col_index * share_cols, 1
    )
    residual = lax.psum((placed - partial_sum).astype(jnp.bfloat16), "col").astype(jnp.float32)
    if across_groups:
        residual = lax.psum(residual.astype(jnp.bfloat16), "gz").astype(jnp.float32)
    result = inverse_rows(residual, inverse)
    return result


def column_vectors(rounded, col_blocks):
    col_index = lax.axis_index("col")
    every_block = lax.all_gather(rounded, "row", axis=0, tiled=True)
    result = lax.dynamic_slice_in_dim(every_block, col_index * col_blocks, col_blocks, 0)
    return result


def back_solve(back_part, solved_rows, inverse, share_cols):
    row_blocks = solved_rows.shape[0]
    summed = lax.psum(back_part.astype(jnp.bfloat16), "row").astype(jnp.float32)
    every_block = lax.all_gather(summed.astype(jnp.bfloat16), "col", axis=0, tiled=True).astype(
        summed.dtype
    )
    own_rows = lax.dynamic_slice_in_dim(
        every_block, lax.axis_index("row") * row_blocks, row_blocks, 0
    )
    answer = inverse_cols(solved_rows - own_rows, inverse)
    share = own_share(answer, share_cols)
    half = answer.astype(jnp.bfloat16)
    return (share, half)


def per_device(
    rhs_sub,
    rhs_top,
    lower_sub,
    lower_link,
    lower_top,
    inv_sub,
    inv_top,
    mask_sub,
    mask_link,
    mask_top,
):
    sub_levels = inv_sub.shape[1]
    top_levels = inv_top.shape[0]
    col_blocks = lower_top.shape[2]
    share_cols = rhs_top.shape[2]
    group_gate = (lax.axis_index("gz") == 0).astype(jnp.float32)
    unit_gate = jnp.float32(1.0)
    row_shape = (inv_top.shape[1], share_cols * lax.axis_size("col"), inv_top.shape[-1])
    column_shape = (col_blocks, row_shape[1], row_shape[2])
    sub_solved = []
    sub_columns = []
    for tier_index in range(sub_levels):
        partial_sum = jnp.zeros(row_shape, jnp.float32)
        for earlier in range(tier_index):
            pair_index = tier_index * (tier_index - 1) // 2 + earlier
            partial_sum = partial_sum + forward_terms(
                sub_columns[earlier], lower_sub[0, pair_index], mask_sub[0, pair_index]
            )
        solved = level_solve(
            partial_sum, rhs_sub[0, tier_index], inv_sub[0, tier_index], unit_gate, False
        )
        sub_solved.append(solved)
        sub_columns.append(column_vectors(solved.astype(jnp.bfloat16), col_blocks))
    top_solved = []
    top_columns = []
    for top_level in range(top_levels):
        partial_sum = forward_terms(
            sub_columns[sub_levels - 1], lower_link[0, top_level], mask_link[0, top_level]
        )
        for earlier in range(top_level):
            pair_index = top_level * (top_level - 1) // 2 + earlier
            partial_sum = partial_sum + group_gate * forward_terms(
                top_columns[earlier], lower_top[pair_index], mask_top[pair_index]
            )
        solved = level_solve(partial_sum, rhs_top[top_level], inv_top[top_level], group_gate, True)
        top_solved.append(solved)
        if top_level + 1 < top_levels:
            top_columns.append(column_vectors(solved.astype(jnp.bfloat16), col_blocks))
    top_share = [None] * top_levels
    top_half = [None] * top_levels
    for top_level in reversed(range(top_levels)):
        if top_level + 1 == top_levels:
            answer = inverse_cols(top_solved[top_level], inv_top[top_level])
            share = own_share(answer, share_cols)
            half = answer.astype(jnp.bfloat16)
        else:
            later_level = 1
            pair_index = later_level * (later_level - 1) // 2 + top_level
            back_part = backward_terms(
                top_half[later_level], lower_top[pair_index], mask_top[pair_index]
            )
            share, half = back_solve(
                back_part, top_solved[top_level], inv_top[top_level], share_cols
            )
        top_share[top_level] = share
        top_half[top_level] = half
    sub_share = [None] * sub_levels
    sub_half = [None] * sub_levels
    for tier_index in reversed(range(sub_levels)):
        back_part = jnp.zeros(column_shape, jnp.float32)
        for later_level in range(tier_index + 1, sub_levels):
            pair_index = later_level * (later_level - 1) // 2 + tier_index
            back_part = back_part + backward_terms(
                sub_half[later_level], lower_sub[0, pair_index], mask_sub[0, pair_index]
            )
        if tier_index == sub_levels - 1:
            for top_level in range(top_levels):
                back_part = back_part + backward_terms(
                    top_half[top_level], lower_link[0, top_level], mask_link[0, top_level]
                )
        share, half = back_solve(
            back_part, sub_solved[tier_index], inv_sub[0, tier_index], share_cols
        )
        sub_share[tier_index] = share
        sub_half[tier_index] = half
    sol_sub = jnp.stack(sub_share)[None]
    sol_top = jnp.stack(top_share)
    return (sol_sub, sol_top)


def solution(mesh):
    return jax.shard_map(
        per_device,
        mesh=mesh,
        in_specs=(
            P("gz", None, "row", "col", None),
            P(None, "row", "col", None),
            P("gz", None, "row", "col", None, None),
            P("gz", None, "row", "col", None, None),
            P(None, "row", "col", None, None),
            P("gz", None, "row", None, None),
            P(None, "row", None, None),
            P("gz", None, "row", "col"),
            P("gz", None, "row", "col"),
            P(None, "row", "col"),
        ),
        out_specs=(P("gz", None, "row", "col", None), P(None, "row", "col", None)),
        check_vma=False,
    )
```

profile of v0, /device:TPU:0, one launch (start us, length us, event | category | flops | bytes accessed | tf_op | source)
XLA Modules:
  0.0 261.6 jit_solution(2911516491720442301)
XLA Ops:
  0.7 0.8 bitcast_dynamic-update-slice_fusion.4
  1.5 21.3 %psum.77 = bf16[96,256]{1,0:T(8,128)(2,1)S(1)} all-reduce(bf16[96,256]{1,0:T(8,128)(2,1)S(1)} %convert_bitcast_fusion), channel_id=1, replica_groups=mesh['gz'=2,'row'=4,'col'=4] {'col'}, use_global_device_ids=true, to_apply=%region_0.0 | all-reduce | flops 24576 | bytes 98304 | tf_op jit(solution)/shard_map/psum | solution.py:41
  22.8 0.2 fusion.124
  22.9 8.7 %all-gather = bf16[384,256]{1,0:T(8,128)(2,1)S(1)} all-gather(bf16[96,256]{1,0:T(8,128)(2,1)S(1)} %get-tuple-element.7), channel_id=2, replica_groups=mesh['gz'=2,'row'=4,'col'=4] {'row'}, dimensions={0}, use_global_device_ids=true | all-gather | bytes 245760 | tf_op jit(solution)/shard_map/all_gather | solution.py:50
  31.7 0.9 copy-done.5
  32.6 0.6 copy-done.7
  33.2 0.6 fusion.123
  34.5 0.2 fusion.26
  34.6 16.1 %psum.78 = bf16[96,256]{1,0:T(8,128)(2,1)S(1)} all-reduce(bf16[96,256]{1,0:T(8,128)(2,1)S(1)} %fusion.26), channel_id=1, replica_groups=mesh['gz'=2,'row'=4,'col'=4] {'col'}, use_global_device_ids=true, to_apply=%region_1.0 | all-reduce | flops 24576 | bytes 98304 | tf_op jit(solution)/shard_map/psum | solution.py:41
  50.7 0.2 fusion.125
  50.9 8.7 %all-gather.1 = bf16[384,256]{1,0:T(8,128)(2,1)S(1)} all-gather(bf16[96,256]{1,0:T(8,128)(2,1)S(1)} %get-tuple-element.9), channel_id=3, replica_groups=mesh['gz'=2,'row'=4,'col'=4] {'row'}, dimensions={0}, use_global_device_ids=true | all-gather | bytes 245760 | tf_op jit(solution)/shard_map/all_gather | solution.py:50
  60.2 0.2 convolution_multiply_fusion.9
  61.0 0.2 fusion.27
  61.2 18.0 %psum.79 = bf16[96,256]{1,0:T(8,128)(2,1)S(1)} all-reduce(bf16[96,256]{1,0:T(8,128)(2,1)S(1)} %fusion.27), channel_id=1, replica_groups=mesh['gz'=2,'row'=4,'col'=4] {'col'}, use_global_device_ids=true, to_apply=%region_2.0 | all-reduce | flops 24576 | bytes 98304 | tf_op jit(solution)/shard_map/psum | solution.py:41
  79.2 0.2 fusion.126
  79.4 7.9 %all-gather.2 = bf16[384,256]{1,0:T(8,128)(2,1)S(1)} all-gather(bf16[96,256]{1,0:T(8,128)(2,1)S(1)} %get-tuple-element.11), channel_id=4, replica_groups=mesh['gz'=2,'row'=4,'col'=4] {'row'}, dimensions={0}, use_global_device_ids=true | all-gather | bytes 245760 | tf_op jit(solution)/shard_map/all_gather | solution.py:50
  87.2 0.8 copy-done.6
  88.0 0.6 copy-done.8
  88.7 0.6 fusion.122
  90.0 0.2 fusion.17
  90.2 16.1 %psum.80 = bf16[1,96,256]{2,1,0:T(8,128)(2,1)S(1)} all-reduce(bf16[1,96,256]{2,1,0:T(8,128)(2,1)S(1)} %fusion.17), channel_id=1, replica_groups=mesh['gz'=2,'row'=4,'col'=4] {'col'}, use_global_device_ids=true, to_apply=%region_3.0 | all-reduce | flops 24576 | bytes 98304 | tf_op jit(solution)/shard_map/psum | solution.py:41
  106.3 3.5 %psum.81 = bf16[96,256]{1,0:T(8,128)(2,1)S(1)} all-reduce(bf16[96,256]{1,0:T(8,128)(2,1)S(1)} %bitcast.253), channel_id=1, replica_groups=mesh['gz'=2,'row'=4,'col'=4] {'gz'}, use_global_device_ids=true, to_apply=%region_4.0 | all-reduce | flops 24576 | bytes 98304 | tf_op jit(solution)/shard_map/psum | solution.py:43
  110.0 8.7 %all-gather.3 = bf16[384,256]{1,0:T(8,128)(2,1)S(1)} all-gather(bf16[96,256]{1,0:T(8,128)(2,1)S(1)} %get-tuple-element.13), channel_id=5, replica_groups=mesh['gz'=2,'row'=4,'col'=4] {'row'}, dimensions={0}, use_global_device_ids=true | all-gather | bytes 245760 | tf_op jit(solution)/shard_map/all_gather | solution.py:50
  119.4 0.2 fusion.6
  120.2 0.2 fusion.16
  120.4 18.0 %psum.82 = bf16[1,96,256]{2,1,0:T(8,128)(2,1)S(1)} all-reduce(bf16[1,96,256]{2,1,0:T(8,128)(2,1)S(1)} %fusion.16), channel_id=1, replica_groups=mesh['gz'=2,'row'=4,'col'=4] {'col'}, use_global_device_ids=true, to_apply=%region_5.0 | all-reduce | flops 24576 | bytes 98304 | tf_op jit(solution)/shard_map/psum | solution.py:41
  138.4 3.5 %psum.83 = bf16[96,256]{1,0:T(8,128)(2,1)S(1)} all-reduce(bf16[96,256]{1,0:T(8,128)(2,1)S(1)} %bitcast.254), channel_id=1, replica_groups=mesh['gz'=2,'row'=4,'col'=4] {'gz'}, use_global_device_ids=true, to_apply=%region_6.0 | all-reduce | flops 24576 | bytes 98304 | tf_op jit(solution)/shard_map/psum | solution.py:43
  142.0 0.3 fusion.21
  142.3 0.2 fusion.23
  142.5 15.8 %psum.84 = bf16[1,96,256]{2,1,0:T(8,128)(2,1)S(1)} all-reduce(bf16[1,96,256]{2,1,0:T(8,128)(2,1)S(1)} %fusion.23), channel_id=1, replica_groups=mesh['gz'=2,'row'=4,'col'=4] {'row'}, use_global_device_ids=true, to_apply=%region_7.0 | all-reduce | flops 24576 | bytes 98304 | tf_op jit(solution)/shard_map/psum | solution.py:57
  158.3 13.7 %all_gather.28 = bf16[4,96,256]{2,1,0:T(8,128)(2,1)S(1)} all-gather(bf16[1,96,256]{2,1,0:T(8,128)(2,1)S(1)} %psum.84), channel_id=1, replica_groups=mesh['gz'=2,'row'=4,'col'=4] {'col'}, dimensions={0}, use_global_device_ids=true | all-gather | bytes 245760 | tf_op jit(solution)/shard_map/all_gather | solution.py:58
  172.0 0.2 fusion.34
  172.2 0.6 pad_maximum_fusion
  172.8 0.2 convolution_multiply_fusion.3
  173.0 0.2 fusion.24
  173.2 14.7 %psum.85 = bf16[1,96,256]{2,1,0:T(8,128)(2,1)S(1)} all-reduce(bf16[1,96,256]{2,1,0:T(8,128)(2,1)S(1)} %fusion.24), channel_id=1, replica_groups=mesh['gz'=2,'row'=4,'col'=4] {'row'}, use_global_device_ids=true, to_apply=%region_8.0 | all-reduce | flops 24576 | bytes 98304 | tf_op jit(solution)/shard_map/psum | solution.py:57
  187.9 13.6 %all_gather.29 = bf16[4,96,256]{2,1,0:T(8,128)(2,1)S(1)} all-gather(bf16[1,96,256]{2,1,0:T(8,128)(2,1)S(1)} %psum.85), channel_id=1, replica_groups=mesh['gz'=2,'row'=4,'col'=4] {'col'}, dimensions={0}, use_global_device_ids=true | all-gather | bytes 245760 | tf_op jit(solution)/shard_map/all_gather | solution.py:58
  201.5 0.2 fusion.40
  201.7 0.2 fusion.22
  201.9 15.7 %psum.86 = bf16[1,96,256]{2,1,0:T(8,128)(2,1)S(1)} all-reduce(bf16[1,96,256]{2,1,0:T(8,128)(2,1)S(1)} %fusion.22), channel_id=1, replica_groups=mesh['gz'=2,'row'=4,'col'=4] {'row'}, use_global_device_ids=true, to_apply=%region_9.0 | all-reduce | flops 24576 | bytes 98304 | tf_op jit(solution)/shard_map/psum | solution.py:57
  217.6 13.8 %all_gather.30 = bf16[4,96,256]{2,1,0:T(8,128)(2,1)S(1)} all-gather(bf16[1,96,256]{2,1,0:T(8,128)(2,1)S(1)} %psum.86), channel_id=1, replica_groups=mesh['gz'=2,'row'=4,'col'=4] {'col'}, dimensions={0}, use_global_device_ids=true | all-gather | bytes 245760 | tf_op jit(solution)/shard_map/all_gather | solution.py:58
  231.4 0.2 fusion.48
  231.5 0.2 convolution_multiply_fusion
  231.8 0.2 fusion.25
  232.0 15.2 %psum.87 = bf16[1,96,256]{2,1,0:T(8,128)(2,1)S(1)} all-reduce(bf16[1,96,256]{2,1,0:T(8,128)(2,1)S(1)} %fusion.25), channel_id=1, replica_groups=mesh['gz'=2,'row'=4,'col'=4] {'row'}, use_global_device_ids=true, to_apply=%region_10.0 | all-reduce | flops 24576 | bytes 98304 | tf_op jit(solution)/shard_map/psum | solution.py:57
  247.2 13.6 %all_gather.31 = bf16[4,96,256]{2,1,0:T(8,128)(2,1)S(1)} all-gather(bf16[1,96,256]{2,1,0:T(8,128)(2,1)S(1)} %psum.87), channel_id=1, replica_groups=mesh['gz'=2,'row'=4,'col'=4] {'col'}, dimensions={0}, use_global_device_ids=true | all-gather | bytes 245760 | tf_op jit(solution)/shard_map/all_gather | solution.py:58
  260.8 0.2 fusion.54
  261.0 0.6 maximum_bitcast_fusion
  (30 shorter events, 0.4 us)
Async XLA Ops:
  0.6 118.7 %copy-start = (bf16[1,1,1,256,256]{4,3,2,1,0:T(8,128)(2,1)S(1)}, bf16[1,1,1,256,256]{4,3,2,1,0:T(8,128)(2,1)}, u32[]{:S(2)}) copy-start(bf16[1,1,1,256,256]{4,3,2,1,0:T(8,128)(2,1)} %param.14) | copy-start | bytes 393220
  0.6 22.1 %copy-start.2 = (bf16[1,3,1,256,256]{4,3,2,1,0:T(8,128)(2,1)S(1)}, bf16[1,3,1,256,256]{4,3,2,1,0:T(8,128)(2,1)}, u32[]{:S(2)}) copy-start(bf16[1,3,1,256,256]{4,3,2,1,0:T(8,128)(2,1)} %param.15) | copy-start | bytes 1179652
  22.8 11.7 %copy-start.1 = (bf16[1,3,1,1,256,256]{5,4,3,2,1,0:T(8,128)(2,1)S(1)}, bf16[1,3,1,1,256,256]{5,4,3,2,1,0:T(8,128)(2,1)}, u32[]{:S(2)}) copy-start(bf16[1,3,1,1,256,256]{5,4,3,2,1,0:T(8,128)(2,1)} %param.12) | copy-start | bytes 1179652
  31.7 0.9 copy-start.5
  32.6 0.7 copy-start.7
  79.4 10.6 %copy-start.3 = (bf16[1,2,1,1,256,256]{5,4,3,2,1,0:T(8,128)(2,1)S(1)}, bf16[1,2,1,1,256,256]{5,4,3,2,1,0:T(8,128)(2,1)}, u32[]{:S(2)}) copy-start(bf16[1,2,1,1,256,256]{5,4,3,2,1,0:T(8,128)(2,1)} %param.13) | copy-start | bytes 786436
  87.2 0.8 copy-start.6
  88.0 0.7 copy-start.8
  90.0 19.8 %copy-start.4 = (bf16[2,1,256,256]{3,2,1,0:T(8,128)(2,1)S(1)}, bf16[2,1,256,256]{3,2,1,0:T(8,128)(2,1)}, u32[]{:S(2)}) copy-start(bf16[2,1,256,256]{3,2,1,0:T(8,128)(2,1)} %param.16) | copy-start | bytes 786436
where the time goes:
time: 262 us
  blocking collectives  247 us (94%)
  local copies, waits for them, and re-layouts  5.17 us (2%)
  between operations  4.84 us (2%)
  matrix products  3.7 us (1%)
    psum x5, blocking collectives, level_solve(): lax.psum((placed - partial_sum).astype(jnp.bfloat16), 'col')  89.5 us
    psum x4, blocking collectives, back_solve(): summed = lax.psum(back_part.astype(jnp.bfloat16), 'row').astype(jnp.float32)  61.4 us
    all_gather x4, blocking collectives, back_solve(): lax.all_gather(summed.astype(jnp.bfloat16), 'col', axis=0, tiled=True)  54.6 us
    all_gather x4, blocking collectives, column_vectors(): every_block = lax.all_gather(rounded, 'row', axis=0, tiled=True)  34 us
    psum x2, blocking collectives, level_solve(): residual = lax.psum(residual.astype(jnp.bfloat16), 'gz').astype(jnp.float32)  7.06 us

commit v1 on v0

--- a/solution.py
+++ b/solution.py
@@ -38,7 +38,9 @@
     placed = lax.dynamic_update_slice_in_dim(
         jnp.zeros_like(partial_sum), rhs_local * gate_value, col_index * share_cols, 1
     )
-    residual = lax.psum((placed - partial_sum).astype(jnp.bfloat16), "col").astype(jnp.float32)
+    residual = jnp.sum(
+        lax.all_gather((placed - partial_sum).astype(jnp.bfloat16), "col"), axis=0
+    ).astype(jnp.float32)
     if across_groups:
         residual = lax.psum(residual.astype(jnp.bfloat16), "gz").astype(jnp.float32)
     result = inverse_rows(residual, inverse)

time: 262 us -> 243 us (0.927)
  blocking collectives: 247 us -> 228 us
    psum x5 -> x0, blocking collectives: 89.5 us -> none  [level_solve(): lax.psum((placed - partial_sum).astype(jnp.bfloat16), 'col')]
    all_gather x0 -> x5, blocking collectives: none -> 70.5 us  [level_solve(): lax.all_gather((placed - partial_sum).astype(jnp.bfloat16), 'col')]
where the time goes in v1:
time: 243 us
  blocking collectives  228 us (94%)
  between operations  4.84 us (2%)
  local copies, waits for them, and re-layouts  4.37 us (2%)
  matrix products  3.7 us (2%)
    all_gather x5, blocking collectives, level_solve(): lax.all_gather((placed - partial_sum).astype(jnp.bfloat16), 'col')  70.5 us
    psum x4, blocking collectives, back_solve(): summed = lax.psum(back_part.astype(jnp.bfloat16), 'row').astype(jnp.float32)  61.7 us
    all_gather x4, blocking collectives, back_solve(): lax.all_gather(summed.astype(jnp.bfloat16), 'col', axis=0, tiled=True)  54.9 us
    all_gather x4, blocking collectives, column_vectors(): every_block = lax.all_gather(rounded, 'row', axis=0, tiled=True)  33.9 us
    psum x2, blocking collectives, level_solve(): residual = lax.psum(residual.astype(jnp.bfloat16), 'gz').astype(jnp.float32)  7.06 us

profile of v1, /device:TPU:0, one launch (start us, length us, event | category | flops | bytes accessed | tf_op | source)
XLA Modules:
  0.0 242.5 jit_solution(9831118319393868933)
XLA Ops:
  0.7 0.9 copy-done.5
  1.6 15.5 %all-gather = bf16[4,96,256]{2,1,0:T(8,128)(2,1)S(1)} all-gather(bf16[1,96,256]{2,1,0:T(8,128)(2,1)S(1)} %convert_element_type.230), channel_id=2, replica_groups=mesh['gz'=2,'row'=4,'col'=4] {'col'}, dimensions={0}, use_global_device_ids=true | all-gather | bytes 245760 | tf_op jit(solution)/shard_map/all_gather | solution.py:42
  17.1 0.2 fusion.122
  17.3 8.7 %all-gather.1 = bf16[384,256]{1,0:T(8,128)(2,1)S(1)} all-gather(bf16[96,256]{1,0:T(8,128)(2,1)S(1)} %get-tuple-element.7), channel_id=3, replica_groups=mesh['gz'=2,'row'=4,'col'=4] {'row'}, dimensions={0}, use_global_device_ids=true | all-gather | bytes 245760 | tf_op jit(solution)/shard_map/all_gather | solution.py:52
  26.0 0.6 copy-done.7
  26.7 0.6 fusion.121
  27.9 0.2 fusion.18
  28.1 13.9 %all-gather.2 = bf16[4,96,256]{2,1,0:T(8,128)(2,1)S(1)} all-gather(bf16[1,96,256]{2,1,0:T(8,128)(2,1)S(1)} %fusion.18), channel_id=4, replica_groups=mesh['gz'=2,'row'=4,'col'=4] {'col'}, dimensions={0}, use_global_device_ids=true | all-gather | bytes 245760 | tf_op jit(solution)/shard_map/all_gather | solution.py:42
  42.0 0.2 fusion.123
  42.1 8.7 %all-gather.3 = bf16[384,256]{1,0:T(8,128)(2,1)S(1)} all-gather(bf16[96,256]{1,0:T(8,128)(2,1)S(1)} %get-tuple-element.9), channel_id=5, replica_groups=mesh['gz'=2,'row'=4,'col'=4] {'row'}, dimensions={0}, use_global_device_ids=true | all-gather | bytes 245760 | tf_op jit(solution)/shard_map/all_gather | solution.py:52
  51.4 0.2 convolution_multiply_fusion.9
  52.3 0.2 fusion.15
  52.4 13.7 %all-gather.4 = bf16[4,96,256]{2,1,0:T(8,128)(2,1)S(1)} all-gather(bf16[1,96,256]{2,1,0:T(8,128)(2,1)S(1)} %fusion.15), channel_id=6, replica_groups=mesh['gz'=2,'row'=4,'col'=4] {'col'}, dimensions={0}, use_global_device_ids=true | all-gather | bytes 245760 | tf_op jit(solution)/shard_map/all_gather | solution.py:42
  66.1 0.2 fusion.124
  66.3 7.9 %all-gather.5 = bf16[384,256]{1,0:T(8,128)(2,1)S(1)} all-gather(bf16[96,256]{1,0:T(8,128)(2,1)S(1)} %get-tuple-element.11), channel_id=7, replica_groups=mesh['gz'=2,'row'=4,'col'=4] {'row'}, dimensions={0}, use_global_device_ids=true | all-gather | bytes 245760 | tf_op jit(solution)/shard_map/all_gather | solution.py:52
  74.2 0.8 copy-done.6
  75.0 0.6 copy-done.8
  75.6 0.6 fusion.120
  77.0 0.2 fusion.17
  77.1 13.8 %all-gather.6 = bf16[4,96,256]{2,1,0:T(8,128)(2,1)S(1)} all-gather(bf16[1,96,256]{2,1,0:T(8,128)(2,1)S(1)} %fusion.17), channel_id=8, replica_groups=mesh['gz'=2,'row'=4,'col'=4] {'col'}, dimensions={0}, use_global_device_ids=true | all-gather | bytes 245760 | tf_op jit(solution)/shard_map/all_gather | solution.py:42
  91.0 3.5 %psum.42 = bf16[96,256]{1,0:T(8,128)(2,1)S(1)} all-reduce(bf16[96,256]{1,0:T(8,128)(2,1)S(1)} %reduce.13), channel_id=1, replica_groups=mesh['gz'=2,'row'=4,'col'=4] {'gz'}, use_global_device_ids=true, to_apply=%region_4.0 | all-reduce | flops 24576 | bytes 98304 | tf_op jit(solution)/shard_map/psum | solution.py:45
  94.5 0.2 fusion.125
  94.7 8.6 %all-gather.7 = bf16[384,256]{1,0:T(8,128)(2,1)S(1)} all-gather(bf16[96,256]{1,0:T(8,128)(2,1)S(1)} %get-tuple-element.13), channel_id=9, replica_groups=mesh['gz'=2,'row'=4,'col'=4] {'row'}, dimensions={0}, use_global_device_ids=true | all-gather | bytes 245760 | tf_op jit(solution)/shard_map/all_gather | solution.py:52
  104.0 0.2 fusion.6
  104.8 0.2 fusion.16
  105.0 13.7 %all-gather.8 = bf16[4,96,256]{2,1,0:T(8,128)(2,1)S(1)} all-gather(bf16[1,96,256]{2,1,0:T(8,128)(2,1)S(1)} %fusion.16), channel_id=10, replica_groups=mesh['gz'=2,'row'=4,'col'=4] {'col'}, dimensions={0}, use_global_device_ids=true | all-gather | bytes 245760 | tf_op jit(solution)/shard_map/all_gather | solution.py:42
  118.7 3.5 %psum.43 = bf16[96,256]{1,0:T(8,128)(2,1)S(1)} all-reduce(bf16[96,256]{1,0:T(8,128)(2,1)S(1)} %reduce.14), channel_id=1, replica_groups=mesh['gz'=2,'row'=4,'col'=4] {'gz'}, use_global_device_ids=true, to_apply=%region_6.0 | all-reduce | flops 24576 | bytes 98304 | tf_op jit(solution)/shard_map/psum | solution.py:45
  122.3 0.3 fusion.21
  122.6 0.2 fusion.23
  122.8 15.8 %psum.44 = bf16[1,96,256]{2,1,0:T(8,128)(2,1)S(1)} all-reduce(bf16[1,96,256]{2,1,0:T(8,128)(2,1)S(1)} %fusion.23), channel_id=1, replica_groups=mesh['gz'=2,'row'=4,'col'=4] {'row'}, use_global_device_ids=true, to_apply=%region_7.0 | all-reduce | flops 24576 | bytes 98304 | tf_op jit(solution)/shard_map/psum | solution.py:59
  138.6 14.0 %all_gather.68 = bf16[4,96,256]{2,1,0:T(8,128)(2,1)S(1)} all-gather(bf16[1,96,256]{2,1,0:T(8,128)(2,1)S(1)} %psum.44), channel_id=1, replica_groups=mesh['gz'=2,'row'=4,'col'=4] {'col'}, dimensions={0}, use_global_device_ids=true | all-gather | bytes 245760 | tf_op jit(solution)/shard_map/all_gather | solution.py:60
  152.6 0.2 fusion.32
  152.8 0.6 pad_maximum_fusion
  153.4 0.2 convolution_multiply_fusion.3
  153.6 0.2 fusion.24
  153.8 14.7 %psum.45 = bf16[1,96,256]{2,1,0:T(8,128)(2,1)S(1)} all-reduce(bf16[1,96,256]{2,1,0:T(8,128)(2,1)S(1)} %fusion.24), channel_id=1, replica_groups=mesh['gz'=2,'row'=4,'col'=4] {'row'}, use_global_device_ids=true, to_apply=%region_8.0 | all-reduce | flops 24576 | bytes 98304 | tf_op jit(solution)/shard_map/psum | solution.py:59
  168.6 13.6 %all_gather.69 = bf16[4,96,256]{2,1,0:T(8,128)(2,1)S(1)} all-gather(bf16[1,96,256]{2,1,0:T(8,128)(2,1)S(1)} %psum.45), channel_id=1, replica_groups=mesh['gz'=2,'row'=4,'col'=4] {'col'}, dimensions={0}, use_global_device_ids=true | all-gather | bytes 245760 | tf_op jit(solution)/shard_map/all_gather | solution.py:60
  182.1 0.2 fusion.38
  182.3 0.2 fusion.22
  182.5 15.8 %psum.46 = bf16[1,96,256]{2,1,0:T(8,128)(2,1)S(1)} all-reduce(bf16[1,96,256]{2,1,0:T(8,128)(2,1)S(1)} %fusion.22), channel_id=1, replica_groups=mesh['gz'=2,'row'=4,'col'=4] {'row'}, use_global_device_ids=true, to_apply=%region_9.0 | all-reduce | flops 24576 | bytes 98304 | tf_op jit(solution)/shard_map/psum | solution.py:59
  198.3 13.7 %all_gather.70 = bf16[4,96,256]{2,1,0:T(8,128)(2,1)S(1)} all-gather(bf16[1,96,256]{2,1,0:T(8,128)(2,1)S(1)} %psum.46), channel_id=1, replica_groups=mesh['gz'=2,'row'=4,'col'=4] {'col'}, dimensions={0}, use_global_device_ids=true | all-gather | bytes 245760 | tf_op jit(solution)/shard_map/all_gather | solution.py:60
  212.0 0.2 fusion.46
  212.1 0.2 convolution_multiply_fusion
  212.3 0.2 fusion.25
  212.5 15.4 %psum.47 = bf16[1,96,256]{2,1,0:T(8,128)(2,1)S(1)} all-reduce(bf16[1,96,256]{2,1,0:T(8,128)(2,1)S(1)} %fusion.25), channel_id=1, replica_groups=mesh['gz'=2,'row'=4,'col'=4] {'row'}, use_global_device_ids=true, to_apply=%region_10.0 | all-reduce | flops 24576 | bytes 98304 | tf_op jit(solution)/shard_map/psum | solution.py:59
  227.9 13.7 %all_gather.71 = bf16[4,96,256]{2,1,0:T(8,128)(2,1)S(1)} all-gather(bf16[1,96,256]{2,1,0:T(8,128)(2,1)S(1)} %psum.47), channel_id=1, replica_groups=mesh['gz'=2,'row'=4,'col'=4] {'col'}, dimensions={0}, use_global_device_ids=true | all-gather | bytes 245760 | tf_op jit(solution)/shard_map/all_gather | solution.py:60
  241.7 0.2 fusion.52
  241.9 0.6 maximum_bitcast_fusion
  (35 shorter events, 0.4 us)
Async XLA Ops:
  0.6 103.3 %copy-start = (bf16[1,1,1,256,256]{4,3,2,1,0:T(8,128)(2,1)S(1)}, bf16[1,1,1,256,256]{4,3,2,1,0:T(8,128)(2,1)}, u32[]{:S(2)}) copy-start(bf16[1,1,1,256,256]{4,3,2,1,0:T(8,128)(2,1)} %param.14) | copy-start | bytes 393220
  0.6 0.9 copy-start.5
  0.7 16.4 %copy-start.2 = (bf16[1,3,1,256,256]{4,3,2,1,0:T(8,128)(2,1)S(1)}, bf16[1,3,1,256,256]{4,3,2,1,0:T(8,128)(2,1)}, u32[]{:S(2)}) copy-start(bf16[1,3,1,256,256]{4,3,2,1,0:T(8,128)(2,1)} %param.15) | copy-start | bytes 1179652
  17.1 10.8 %copy-start.1 = (bf16[1,3,1,1,256,256]{5,4,3,2,1,0:T(8,128)(2,1)S(1)}, bf16[1,3,1,1,256,256]{5,4,3,2,1,0:T(8,128)(2,1)}, u32[]{:S(2)}) copy-start(bf16[1,3,1,1,256,256]{5,4,3,2,1,0:T(8,128)(2,1)} %param.12) | copy-start | bytes 1179652
  26.0 0.7 copy-start.7
  66.3 10.6 %copy-start.3 = (bf16[1,2,1,1,256,256]{5,4,3,2,1,0:T(8,128)(2,1)S(1)}, bf16[1,2,1,1,256,256]{5,4,3,2,1,0:T(8,128)(2,1)}, u32[]{:S(2)}) copy-start(bf16[1,2,1,1,256,256]{5,4,3,2,1,0:T(8,128)(2,1)} %param.13) | copy-start | bytes 786436
  74.2 0.8 copy-start.6
  75.0 0.7 copy-start.8
  77.1 17.4 %copy-start.4 = (bf16[2,1,256,256]{3,2,1,0:T(8,128)(2,1)S(1)}, bf16[2,1,256,256]{3,2,1,0:T(8,128)(2,1)}, u32[]{:S(2)}) copy-start(bf16[2,1,256,256]{3,2,1,0:T(8,128)(2,1)} %param.16) | copy-start | bytes 786436
